TPU v7x, 32 devices: a whole 2x2x4 slice. The times are simulated.
32 devices in a mesh: rows: 8 (over z, y), cols: 4 (over x, core).
Axes of the slice: x: 2, y: 2, z: 4, core: 2. Of those that a mesh axis runs over, the one named last changes fastest.
Arguments:
- features: bfloat16 [64, 512, 512], P('rows', 'cols'), may hold values from -6 to 6
- dw_weight: float32 [49, 512], replicated, may hold values from -0.875 to 0.875
- norm_gain: float32 [512], replicated, may hold values from 0.1 to 1.9
- w_up: bfloat16 [512, 2048], replicated, may hold values from -0.25 to 0.25
- w_down: bfloat16 [2048, 512], replicated, may hold values from -0.125 to 0.125
- cotangent: bfloat16 [64, 512, 512], P('rows', 'cols'), may hold values from -6 to 6
Outputs:
- grad_input: bfloat16 [64, 512, 512], P('rows', 'cols')
- grad_dw: float32 [49, 512], replicated
- grad_gain: float32 [512], replicated
- grad_up: float32 [512, 2048], replicated
- grad_down: float32 [2048, 512], replicated
All inputs are finite; a program needn't handle non-finite values.
Results may differ from a plain program's by a relative error of at most 0.019.
Values may be sent and summed in bfloat16 or wider, within the bound.
No kernel may reach another device: no remote copies, remote signals or barrier semaphores. Data moves between devices by JAX's collectives and lax.ppermute only.
A program may use at most 128 MiB of HBM per device.

v0:
```python
import jax
import jax.numpy as jnp
from jax import lax
from jax.sharding import PartitionSpec as P

eps = 1e-06


def padded_2(block, sides, width):
    for axis, dim in sides:
        count = lax.axis_size(axis)
        forward = [(i, i + 1) for i in range(count - 1)]
        backward = [(target, source) for source, target in forward]
        low = lax.ppermute(
            lax.slice_in_dim(block, block.shape[dim] - width, None, axis=dim), axis, forward
        )
        high = lax.ppermute(lax.slice_in_dim(block, 0, width, axis=dim), axis, backward)
        block = jnp.concatenate([low, block, high], axis=dim)
    return block


def depthwise(padded, weight, rows, cols):
    total = jnp.zeros((rows, cols, padded.shape[2]), jnp.float32)
    for tap_i in range(7):
        for tap_j in range(7):
            total = (
                total
                + padded[tap_i : tap_i + rows, tap_j : tap_j + cols] * weight[7 * tap_i + tap_j]
            )
    return total


def pointwise(conv, gain, w_up, w_down, grad_out, keep):
    mean = jnp.mean(conv, axis=-1, keepdims=True)
    centred = conv - mean
    inv = lax.rsqrt(jnp.mean(centred * centred, axis=-1, keepdims=True) + eps)
    normed = centred * inv
    scaled = (normed * gain).astype(jnp.bfloat16)
    hidden = jnp.dot(scaled, w_up, preferred_element_type=jnp.float32)
    act = (0.5 * hidden * (1.0 + lax.erf(hidden * 0.7071067811865476))).astype(jnp.bfloat16)
    grad_kept = grad_out * keep.astype(jnp.bfloat16)
    grad_down = lax.dot_general(
        act, grad_kept, (((0,), (0,)), ((), ())), preferred_element_type=jnp.float32
    )
    grad_act = lax.dot_general(
        grad_out, w_down, (((1,), (1,)), ((), ())), preferred_element_type=jnp.float32
    )
    slope = (
        0.5 * (1.0 + lax.erf(hidden * 0.7071067811865476))
        + hidden * jnp.exp(-0.5 * hidden * hidden) * 0.3989422804014327
    )
    grad_hidden = (grad_act * slope).astype(jnp.bfloat16)
    hidden_kept = grad_hidden * keep.astype(jnp.bfloat16)
    grad_up = lax.dot_general(
        scaled, hidden_kept, (((0,), (0,)), ((), ())), preferred_element_type=jnp.float32
    )
    grad_scaled = lax.dot_general(
        grad_hidden, w_up, (((1,), (1,)), ((), ())), preferred_element_type=jnp.float32
    )
    grad_gain = jnp.sum(grad_scaled * normed * keep, axis=0)
    g_norm = grad_scaled * gain
    grad_conv = inv * (
        g_norm
        - jnp.mean(g_norm, axis=-1, keepdims=True)
        - normed * jnp.mean(g_norm * normed, axis=-1, keepdims=True)
    )
    return (grad_conv.astype(jnp.bfloat16), grad_up, grad_down, grad_gain)


def on_device(features, dw_weight, norm_gain, w_up, w_down, cotangent):
    rows, cols, chans = features.shape
    padded = padded_2(features, (("rows", 0), ("cols", 1)), 3).astype(jnp.float32)
    conv = depthwise(padded, dw_weight, rows, cols)
    keep = jnp.ones((rows * cols, 1), jnp.float32)
    grad_flat, grad_up, grad_down, grad_gain = pointwise(
        conv.reshape(rows * cols, chans),
        norm_gain,
        w_up,
        w_down,
        cotangent.reshape(rows * cols, chans),
        keep,
    )
    grad_conv = grad_flat.reshape(rows, cols, chans)
    grad_wide = padded_2(grad_conv, (("rows", 0), ("cols", 1)), 3)
    grad_f = grad_conv.astype(jnp.float32)
    taps = []
    for tap_i in range(7):
        for tap_j in range(7):
            taps.append(
                jnp.sum(padded[tap_i : tap_i + rows, tap_j : tap_j + cols] * grad_f, axis=(0, 1))
            )
    grad_dw = jnp.stack(taps)
    grad_pad = grad_wide.astype(jnp.float32)
    total = cotangent.astype(jnp.float32)
    for tap_i in range(7):
        for tap_j in range(7):
            total = (
                total
                + grad_pad[6 - tap_i : 6 - tap_i + rows, 6 - tap_j : 6 - tap_j + cols]
                * dw_weight[7 * tap_i + tap_j]
            )
    grad_input = total.astype(jnp.bfloat16)
    grad_up, grad_down, grad_dw, grad_gain = lax.psum(
        (grad_up, grad_down, grad_dw, grad_gain), ("rows", "cols")
    )
    return (grad_input, grad_dw, grad_gain, grad_up, grad_down)


def solution(mesh):
    return jax.shard_map(
        on_device,
        mesh=mesh,
        in_specs=(P("rows", "cols", None), P(), P(), P(), P(), P("rows", "cols", None)),
        out_specs=(P("rows", "cols", None), P(), P(), P(), P()),
        check_vma=False,
    )
```

profile of v0, /device:TPU:0, one launch (start us, length us, event | category | flops | bytes accessed | tf_op | source)
XLA Modules:
  0.0 353.4 jit_solution(14381172907683778319)
XLA Ops:
  7.2 0.0 copy-start
  7.2 0.0 copy-start.6
  7.2 0.0 all-reduce.3.cloned.1.call-start
  7.2 1.4 fusion.113
  8.6 4.9 %collective-permute-start = (bf16[3,128,512]{2,1,0:T(8,128)(2,1)S(1)}, bf16[3,128,512]{2,1,0:T(8,128)(2,1)S(1)}, u32[]{:S(2)}, u32[]{:S(2)}) collective-permute-start(bf16[3,128,512]{2,1,0:T(8,128)(2,1)S(1)} %get-tuple-element.70), channel_id=1, source_target_pairs={{0,4},{4,8},{8,12},{12,16},{16,20},{20,24},{24,28},{1,5},{5,9},{9,... | collective-permute-start | bytes 1179656 | tf_op jit(solution)/shard_map/ppermute | solution.py:14
  13.5 1.3 collective-permute-start.1
  14.8 1.1 fusion.114
  16.0 0.0 copy-start.8
  16.0 0.0 copy-start.9
  16.0 0.0 copy-start.10
  16.0 0.0 copy-start.11
  16.1 1.2 fusion.115
  17.5 12.8 %collective-permute-done = bf16[3,128,512]{2,1,0:T(8,128)(2,1)S(1)} collective-permute-done((bf16[3,128,512]{2,1,0:T(8,128)(2,1)S(1)}, bf16[3,128,512]{2,1,0:T(8,128)(2,1)S(1)}, u32[]{:S(2)}, u32[]{:S(2)}) %collective-permute-start) | collective-permute-done | bytes 393248 | tf_op jit(solution)/shard_map/ppermute | solution.py:14
  30.3 0.1 constant_dynamic-update-slice_fusion.1
  30.4 0.0 collective-permute-done.1
  30.5 1.3 collective-permute-start.3
  31.8 3.0 collective-permute-start.2
  34.9 1.6 fusion.116
  36.5 0.0 collective-permute-done.3
  36.5 0.0 collective-permute-done.2
  36.5 2.5 maximum_convert_fusion
  39.1 0.0 copy-done.9
  39.4 54.0 %fusion.110 = (f32[8,128]{1,0:T(8,128)S(1)}, f32[8,128,512]{2,1,0:T(8,128)}) fusion(f32[512]{0:T(512)} %bitcast.48, f32[14,134,512]{2,1,0:T(8,128)} %maximum_convert_fusion, f32[512]{0:T(512)} %bitcast.47, f32[512]{0:T(512)S(1)} %bitcast.183, f32[512]{0:T(512)S(1)} %bitcast.185, f32[512]{0:T(512)S(1)} %bitcast.187, f32[512]{0:T(512)S(1)} %bitcast.189, ...), kind=kLoop, calls=%fused_computation.231 | loop fusion | flops 51379200 | bytes 104962048 | tf_op jit(solution)/shard_map/reduce_sum | solution.py:34
  93.4 0.0 copy-start.2
  93.4 0.0 copy-start.47
  93.4 2.1 multiply_reduce_fusion.2
  95.6 0.0 copy-done.2
  95.6 0.0 copy-done.47
  95.6 0.3 multiply_convert_fusion.3
  96.0 0.0 copy-done
  96.0 0.0 copy-start.4
  96.0 0.0 copy-start.7
  96.0 0.0 copy-start.48
  96.0 2.3 fusion.117
  98.4 5.0 %fusion.5 = bf16[1024,2048]{1,0:T(8,128)(2,1)S(1)} fusion(f32[1024,2048]{1,0:T(8,128)S(1)} %fusion.117, bf16[1024,512]{1,0:T(8,128)(2,1)S(1)} %bitcast.179, bf16[2048,512]{1,0:T(8,128)(2,1)S(1)} %copy-done.48), kind=kOutput, calls=%fused_computation.55 | convolution fusion | flops 2168455168 | bytes 15728640 | tf_op jit(solution)/shard_map/dot_general | solution.py:45
  103.5 0.0 copy-done.49
  103.5 0.0 copy-start.3
  103.5 0.0 copy-start.1
  103.5 3.4 multiply_reduce_fusion
  106.9 0.2 copy-done.1
  107.1 6.6 %fusion.56 = (f32[512]{0:T(512)}, f32[512]{0:T(512)}, f32[512]{0:T(512)}, f32[512]{0:T(512)}, f32[512]{0:T(512)}, /*index=5*/f32[512]{0:T(512)}, f32[512]{0:T(51...) fusion(f32[14,134,512]{2,1,0:T(8,128)S(1)} %copy-done.1, ...), kind=kLoop, calls=%fused_computation.108 | loop fusion | flops 23583744 | bytes 43046912 | tf_op jit(solution)/shard_map/reduce_sum | solution.py:90
  113.7 1.0 fusion.112
  114.7 4.0 %fusion.20 = (f32[512]{0:T(512)}, f32[512]{0:T(512)}, f32[512]{0:T(512)}, f32[512]{0:T(512)}, f32[512]{0:T(512)}, /*index=5*/f32[512]{0:T(512)}, f32[512]{0:T(51...) fusion(f32[14,134,512]{2,1,0:T(8,128)S(1)} %copy-done.1, ...), kind=kLoop, calls=%fused_computation.72 | loop fusion | flops 14149120 | bytes 28338176 | tf_op jit(solution)/shard_map/reduce_sum | solution.py:90
  118.7 5.3 %fusion.38 = (f32[512]{0:T(512)}, f32[512]{0:T(512)}, f32[512]{0:T(512)}, f32[512]{0:T(512)}, f32[512]{0:T(512)}, /*index=5*/f32[512]{0:T(512)}, f32[512]{0:T(51...) fusion(f32[14,134,512]{2,1,0:T(8,128)S(1)} %copy-done.1, ...), kind=kLoop, calls=%fused_computation.90 | loop fusion | flops 19389440 | bytes 38834176 | tf_op jit(solution)/shard_map/reduce_sum | solution.py:90
  124.0 6.1 %fusion.6 = f32[2048,512]{1,0:T(8,128)} fusion(bf16[1024,512]{1,0:T(8,128)(2,1)S(1)} %bitcast.180, f32[1024,2048]{1,0:T(8,128)} %copy-done.49), kind=kOutput, calls=%fused_computation.58 | convolution fusion | flops 2157969408 | bytes 13631488 | tf_op jit(solution)/shard_map/dot_general | solution.py:42
  130.1 1.3 collective-permute-start.5
  131.4 5.8 %collective-permute-start.4 = (bf16[3,128,512]{2,1,0:T(8,128)(2,1)}, bf16[3,128,512]{2,1,0:T(8,128)(2,1)}, u32[]{:S(2)}, u32[]{:S(2)}) collective-permute-start(bf16[3,128,512]{2,1,0:T(8,128)(2,1)} %bitcast.53), channel_id=1, source_target_pairs={{0,4},{4,8},{8,12},{12,16},{16,20},{20,24},{24,28},{1,5},{5,9},{9,... | collective-permute-start | bytes 1179656 | tf_op jit(solution)/shard_map/ppermute | solution.py:14
  137.2 9.4 %stack.199 = f32[49,512]{1,0:T(8,128)} concatenate(f32[1,512]{1,0:T(1,128)} %bitcast.315, f32[1,512]{1,0:T(1,128)} %bitcast.314, f32[1,512]{1,0:T(1,128)} %bitcast.313, f32[1,512]{1,0:T(1,128)} %bitcast.312, f32[1,512]{1,0:T(1,128)} %bitcast.311, f32[1,512]{1,0:T(1,128)} %bitcast.310, f32[1,512]{1,0:T(1,128)} %bitcast.309, f32[1,512]{1,0:T(1,128)} %bitcast.308, ...), dimensions={0} | concatenate | bytes 200704 | tf_op jit(solution)/shard_map/stack | solution.py:92
  146.5 6.9 %fusion.118 = f32[512,2048]{1,0:T(8,128)} fusion(bf16[1024,512]{1,0:T(8,128)(2,1)} %copy-done.4, bf16[1024,2048]{1,0:T(8,128)(2,1)} %copy-done.3), kind=kOutput, calls=%fused_computation.239 | convolution fusion | flops 2147483648 | bytes 9437184 | tf_op jit(solution)/shard_map/dot_general | solution.py:54
  153.4 0.0 all-reduce.3.cloned.1.call-update
  153.5 0.0 collective-permute-done.5
  153.5 0.1 collective-permute-done.4
  153.6 1.4 pad_maximum_fusion.2
  155.1 1.3 collective-permute-start.7
  156.3 3.9 %collective-permute-start.6 = (bf16[14,3,512]{2,1,0:T(4,128)(2,1)}, bf16[14,3,512]{2,1,0:T(4,128)(2,1)}, u32[]{:S(2)}, u32[]{:S(2)}) collective-permute-start(bf16[14,3,512]{2,1,0:T(4,128)(2,1)} %get-tuple-element.63), channel_id=1, source_target_pairs={{0,1},{1,2},{2,3},{4,5},{5,6},{6,7},{8,9},{9,10},{10,11},{12,13},{... | collective-permute-start | bytes 129032 | tf_op jit(solution)/shard_map/ppermute | solution.py:14
  160.2 44.4 %psum.29 = f32[512]{0:T(512)} all-reduce(f32[512]{0:T(512)} %get-tuple-element.54), channel_id=1, replica_groups=mesh['rows'=8,'cols'=4] {'rows','cols'}, use_global_device_ids=true, to_apply=%region_55.0 | all-reduce | flops 512 | bytes 4096 | tf_op jit(solution)/shard_map/psum | solution.py:103
  204.6 0.0 collective-permute-done.7
  204.6 0.0 collective-permute-done.6
  204.6 3.6 %maximum_convert_fusion.1 = f32[14,134,512]{2,1,0:T(8,128)} fusion(bf16[14,3,512]{2,1,0:T(4,128)(2,1)} %collective-permute-done.7, bf16[3,128,512]{2,1,0:T(8,128)(2,1)S(1)} %collective-permute-done.5, bf16[8,128,512]{2,1,0:T(8,128)(2,1)S(1)} %bitcast.178, bf16[3,128,512]{2,1,0:T(8,128)(2,1)} %collective-permute-done.4, ...), kind=kLoop, calls=%fused_computation.217 | loop fusion | flops 9605120 | bytes 5763072 | tf_op jit(solution)/shard_map/convert_element_type | solution.py:93
  208.1 52.3 %fusion.58 = bf16[8,128,512]{2,1,0:T(8,128)(2,1)} fusion(f32[14,134,512]{2,1,0:T(8,128)} %maximum_convert_fusion.1, bf16[8,128,512]{2,1,0:T(8,128)(2,1)} %param.11, f32[512]{0:T(512)} %bitcast.48, f32[512]{0:T(512)} %bitcast.47, f32[512]{0:T(512)S(1)} %bitcast.184, f32[512]{0:T(512)S(1)} %bitcast.186, f32[512]{0:T(512)S(1)} %bitcast.188, f32[512]{0:T(512)} %bitcast.190, ...), kind=kLoop, calls=%fused_computation.111 | loop fusion | flops 52428800 | bytes 104957952 | tf_op jit(solution)/shard_map/convert_element_type | solution.py:102
  260.4 77.8 %all-reduce.3.cloned.1.call-done = (f32[49,512]{1,0:T(8,128)}, f32[512,2048]{1,0:T(8,128)}, f32[2048,512]{1,0:T(8,128)}) async-done(((f32[49,512]{1,0:T(8,128)}, f32[512,2048]{1,0:T(8,128)}, f32[2048,512]{1,0:T(8,128)}), (f32[49,512]{1,0:T(8,128)}, f32[512,2048]{1,0:T(8,128)}, f32[2048,512]{1,0:T(8,128)})) %all-reduce.3.cloned.1.call-update) | async-done | bytes 8488976 | tf_op jit(solution)/shard_map/psum | solution.py:103
  338.2 1.6 copy.16
  339.7 4.8 %copy.17 = f32[512,2048]{1,0:T(8,128)} copy(f32[512,2048]{1,0:T(8,128)} %get-tuple-element.128) | data formatting | bytes 8388608
  344.6 2.0 copy.18
  (87 shorter events, 0.3 us)
Async XLA Ops:
  7.2 88.8 %copy-start = (bf16[512,2048]{1,0:T(8,128)(2,1)S(1)}, bf16[512,2048]{1,0:T(8,128)(2,1)}, u32[]{:S(2)}) copy-start(bf16[512,2048]{1,0:T(8,128)(2,1)} %param.9) | copy-start | bytes 6291460
  7.2 23.1 %copy-start.6 = (bf16[8,128,512]{2,1,0:T(8,128)(2,1)S(1)}, bf16[8,128,512]{2,1,0:T(8,128)(2,1)}, u32[]{:S(2)}) copy-start(bf16[8,128,512]{2,1,0:T(8,128)(2,1)} %param.6) | copy-start | bytes 3145732
  7.2 331.0 %all-reduce.3.cloned.1.call-start = ((), (), s32[]{:S(2)}) async-start(), calls=%async_computation | async-start | bytes 17006592 | tf_op jit(solution)/shard_map/psum | solution.py:103
  8.6 21.7 %collective-permute-start = (bf16[3,128,512]{2,1,0:T(8,128)(2,1)S(1)}, bf16[3,128,512]{2,1,0:T(8,128)(2,1)S(1)}, u32[]{:S(2)}, u32[]{:S(2)}) collective-permute-start(bf16[3,128,512]{2,1,0:T(8,128)(2,1)S(1)} %get-tuple-element.70), channel_id=1, source_target_pairs={{0,4},{4,8},{8,12},{12,16},{16,20},{20,24},{24,28},{1,5},{5,9},{9,... | collective-permute-start | bytes 1179656 | tf_op jit(solution)/shard_map/ppermute | solution.py:14
  13.5 16.9 %collective-permute-start.1 = (bf16[3,128,512]{2,1,0:T(8,128)(2,1)S(1)}, bf16[3,128,512]{2,1,0:T(8,128)(2,1)S(1)}, u32[]{:S(2)}, u32[]{:S(2)}) collective-permute-start(bf16[3,128,512]{2,1,0:T(8,128)(2,1)S(1)} %get-tuple-element.69), channel_id=1, source_target_pairs={{4,0},{8,4},{12,8},{16,12},{20,16},{24,20},{28,24},{5,1},{9,5},{13... | collective-permute-start | bytes 1179656 | tf_op jit(solution)/shard_map/ppermute | solution.py:17
  16.0 23.1 %copy-start.8 = (f32[1,512]{1,0:T(1,128)}, f32[1,512]{1,0:T(1,128)S(1)}, u32[]{:S(2)}) copy-start(f32[1,512]{1,0:T(1,128)S(1)} %get-tuple-element.75) | copy-start | bytes 6148
  16.0 23.1 %copy-start.9 = (f32[1,512]{1,0:T(1,128)}, f32[1,512]{1,0:T(1,128)S(1)}, u32[]{:S(2)}) copy-start(f32[1,512]{1,0:T(1,128)S(1)} %get-tuple-element.76) | copy-start | bytes 6148
  16.0 23.1 %copy-start.10 = (f32[1,512]{1,0:T(1,128)}, f32[1,512]{1,0:T(1,128)S(1)}, u32[]{:S(2)}) copy-start(f32[1,512]{1,0:T(1,128)S(1)} %get-tuple-element.77) | copy-start | bytes 6148
  16.0 23.1 %copy-start.11 = (f32[1,512]{1,0:T(1,128)}, f32[1,512]{1,0:T(1,128)S(1)}, u32[]{:S(2)}) copy-start(f32[1,512]{1,0:T(1,128)S(1)} %get-tuple-element.78) | copy-start | bytes 6148
  16.0 23.1 %copy-start.12 = (f32[1,512]{1,0:T(1,128)}, f32[1,512]{1,0:T(1,128)S(1)}, u32[]{:S(2)}) copy-start(f32[1,512]{1,0:T(1,128)S(1)} %get-tuple-element.79) | copy-start | bytes 6148
  16.0 23.1 %copy-start.13 = (f32[1,512]{1,0:T(1,128)}, f32[1,512]{1,0:T(1,128)S(1)}, u32[]{:S(2)}) copy-start(f32[1,512]{1,0:T(1,128)S(1)} %get-tuple-element.80) | copy-start | bytes 6148
  16.0 23.1 %copy-start.14 = (f32[1,512]{1,0:T(1,128)}, f32[1,512]{1,0:T(1,128)S(1)}, u32[]{:S(2)}) copy-start(f32[1,512]{1,0:T(1,128)S(1)} %get-tuple-element.81) | copy-start | bytes 6148
  16.0 23.1 %copy-start.15 = (f32[1,512]{1,0:T(1,128)}, f32[1,512]{1,0:T(1,128)S(1)}, u32[]{:S(2)}) copy-start(f32[1,512]{1,0:T(1,128)S(1)} %get-tuple-element.82) | copy-start | bytes 6148
  16.0 23.1 %copy-start.16 = (f32[1,512]{1,0:T(1,128)}, f32[1,512]{1,0:T(1,128)S(1)}, u32[]{:S(2)}) copy-start(f32[1,512]{1,0:T(1,128)S(1)} %get-tuple-element.83) | copy-start | bytes 6148
  16.0 23.1 %copy-start.17 = (f32[1,512]{1,0:T(1,128)}, f32[1,512]{1,0:T(1,128)S(1)}, u32[]{:S(2)}) copy-start(f32[1,512]{1,0:T(1,128)S(1)} %get-tuple-element.84) | copy-start | bytes 6148
  16.1 23.1 %copy-start.18 = (f32[1,512]{1,0:T(1,128)}, f32[1,512]{1,0:T(1,128)S(1)}, u32[]{:S(2)}) copy-start(f32[1,512]{1,0:T(1,128)S(1)} %get-tuple-element.85) | copy-start | bytes 6148
  16.1 23.1 %copy-start.19 = (f32[1,512]{1,0:T(1,128)}, f32[1,512]{1,0:T(1,128)S(1)}, u32[]{:S(2)}) copy-start(f32[1,512]{1,0:T(1,128)S(1)} %get-tuple-element.86) | copy-start | bytes 6148
  16.1 23.1 %copy-start.20 = (f32[1,512]{1,0:T(1,128)}, f32[1,512]{1,0:T(1,128)S(1)}, u32[]{:S(2)}) copy-start(f32[1,512]{1,0:T(1,128)S(1)} %get-tuple-element.87) | copy-start | bytes 6148
  16.1 23.1 %copy-start.21 = (f32[1,512]{1,0:T(1,128)}, f32[1,512]{1,0:T(1,128)S(1)}, u32[]{:S(2)}) copy-start(f32[1,512]{1,0:T(1,128)S(1)} %get-tuple-element.88) | copy-start | bytes 6148
  16.1 23.1 %copy-start.22 = (f32[1,512]{1,0:T(1,128)}, f32[1,512]{1,0:T(1,128)S(1)}, u32[]{:S(2)}) copy-start(f32[1,512]{1,0:T(1,128)S(1)} %get-tuple-element.89) | copy-start | bytes 6148
  17.3 21.9 %copy-start.23 = (f32[1,512]{1,0:T(1,128)}, f32[1,512]{1,0:T(1,128)S(1)}, u32[]{:S(2)}) copy-start(f32[1,512]{1,0:T(1,128)S(1)} %get-tuple-element.90) | copy-start | bytes 6148
  17.3 21.9 %copy-start.24 = (f32[1,512]{1,0:T(1,128)}, f32[1,512]{1,0:T(1,128)S(1)}, u32[]{:S(2)}) copy-start(f32[1,512]{1,0:T(1,128)S(1)} %get-tuple-element.91) | copy-start | bytes 6148
  17.3 21.9 %copy-start.25 = (f32[1,512]{1,0:T(1,128)}, f32[1,512]{1,0:T(1,128)S(1)}, u32[]{:S(2)}) copy-start(f32[1,512]{1,0:T(1,128)S(1)} %get-tuple-element.92) | copy-start | bytes 6148
  17.3 21.9 %copy-start.26 = (f32[1,512]{1,0:T(1,128)}, f32[1,512]{1,0:T(1,128)S(1)}, u32[]{:S(2)}) copy-start(f32[1,512]{1,0:T(1,128)S(1)} %get-tuple-element.93) | copy-start | bytes 6148
  17.3 21.9 %copy-start.27 = (f32[1,512]{1,0:T(1,128)}, f32[1,512]{1,0:T(1,128)S(1)}, u32[]{:S(2)}) copy-start(f32[1,512]{1,0:T(1,128)S(1)} %get-tuple-element.94) | copy-start | bytes 6148
  17.3 21.9 %copy-start.28 = (f32[1,512]{1,0:T(1,128)}, f32[1,512]{1,0:T(1,128)S(1)}, u32[]{:S(2)}) copy-start(f32[1,512]{1,0:T(1,128)S(1)} %get-tuple-element.95) | copy-start | bytes 6148
  17.3 21.9 %copy-start.29 = (f32[1,512]{1,0:T(1,128)}, f32[1,512]{1,0:T(1,128)S(1)}, u32[]{:S(2)}) copy-start(f32[1,512]{1,0:T(1,128)S(1)} %get-tuple-element.96) | copy-start | bytes 6148
  17.3 21.9 %copy-start.30 = (f32[1,512]{1,0:T(1,128)}, f32[1,512]{1,0:T(1,128)S(1)}, u32[]{:S(2)}) copy-start(f32[1,512]{1,0:T(1,128)S(1)} %get-tuple-element.97) | copy-start | bytes 6148
  17.4 21.9 %copy-start.31 = (f32[1,512]{1,0:T(1,128)}, f32[1,512]{1,0:T(1,128)S(1)}, u32[]{:S(2)}) copy-start(f32[1,512]{1,0:T(1,128)S(1)} %get-tuple-element.98) | copy-start | bytes 6148
  17.4 21.9 %copy-start.32 = (f32[1,512]{1,0:T(1,128)}, f32[1,512]{1,0:T(1,128)S(1)}, u32[]{:S(2)}) copy-start(f32[1,512]{1,0:T(1,128)S(1)} %get-tuple-element.99) | copy-start | bytes 6148
  17.4 21.9 %copy-start.33 = (f32[1,512]{1,0:T(1,128)}, f32[1,512]{1,0:T(1,128)S(1)}, u32[]{:S(2)}) copy-start(f32[1,512]{1,0:T(1,128)S(1)} %get-tuple-element.100) | copy-start | bytes 6148
  17.4 21.9 %copy-start.34 = (f32[1,512]{1,0:T(1,128)}, f32[1,512]{1,0:T(1,128)S(1)}, u32[]{:S(2)}) copy-start(f32[1,512]{1,0:T(1,128)S(1)} %get-tuple-element.101) | copy-start | bytes 6148
  17.4 21.9 %copy-start.35 = (f32[1,512]{1,0:T(1,128)}, f32[1,512]{1,0:T(1,128)S(1)}, u32[]{:S(2)}) copy-start(f32[1,512]{1,0:T(1,128)S(1)} %get-tuple-element.102) | copy-start | bytes 6148
  17.4 21.9 %copy-start.36 = (f32[1,512]{1,0:T(1,128)}, f32[1,512]{1,0:T(1,128)S(1)}, u32[]{:S(2)}) copy-start(f32[1,512]{1,0:T(1,128)S(1)} %get-tuple-element.103) | copy-start | bytes 6148
  17.4 21.9 %copy-start.37 = (f32[1,512]{1,0:T(1,128)}, f32[1,512]{1,0:T(1,128)S(1)}, u32[]{:S(2)}) copy-start(f32[1,512]{1,0:T(1,128)S(1)} %get-tuple-element.104) | copy-start | bytes 6148
  17.4 21.9 %copy-start.38 = (f32[1,512]{1,0:T(1,128)}, f32[1,512]{1,0:T(1,128)S(1)}, u32[]{:S(2)}) copy-start(f32[1,512]{1,0:T(1,128)S(1)} %get-tuple-element.105) | copy-start | bytes 6148
  17.4 21.9 %copy-start.39 = (f32[1,512]{1,0:T(1,128)}, f32[1,512]{1,0:T(1,128)S(1)}, u32[]{:S(2)}) copy-start(f32[1,512]{1,0:T(1,128)S(1)} %get-tuple-element.106) | copy-start | bytes 6148
  17.4 21.9 %copy-start.40 = (f32[1,512]{1,0:T(1,128)}, f32[1,512]{1,0:T(1,128)S(1)}, u32[]{:S(2)}) copy-start(f32[1,512]{1,0:T(1,128)S(1)} %get-tuple-element.107) | copy-start | bytes 6148
  17.5 21.9 %copy-start.41 = (f32[1,512]{1,0:T(1,128)}, f32[1,512]{1,0:T(1,128)S(1)}, u32[]{:S(2)}) copy-start(f32[1,512]{1,0:T(1,128)S(1)} %get-tuple-element.108) | copy-start | bytes 6148
  30.5 6.0 %collective-permute-start.3 = (bf16[14,3,512]{2,1,0:T(4,128)(2,1)S(1)}, bf16[14,3,512]{2,1,0:T(4,128)(2,1)S(1)}, u32[]{:S(2)}, u32[]{:S(2)}) collective-permute-start(bf16[14,3,512]{2,1,0:T(4,128)(2,1)S(1)} %get-tuple-element.66), channel_id=1, source_target_pairs={{1,0},{2,1},{3,2},{5,4},{6,5},{7,6},{9,8},{10,9},{11,10},{13,12},{... | collective-permute-start | bytes 129032 | tf_op jit(solution)/shard_map/ppermute | solution.py:17
  31.8 4.7 %collective-permute-start.2 = (bf16[14,3,512]{2,1,0:T(4,128)(2,1)S(1)}, bf16[14,3,512]{2,1,0:T(4,128)(2,1)S(1)}, u32[]{:S(2)}, u32[]{:S(2)}) collective-permute-start(bf16[14,3,512]{2,1,0:T(4,128)(2,1)S(1)} %get-tuple-element.65), channel_id=1, source_target_pairs={{0,1},{1,2},{2,3},{4,5},{5,6},{6,7},{8,9},{9,10},{10,11},{12,13},{... | collective-permute-start | bytes 129032 | tf_op jit(solution)/shard_map/ppermute | solution.py:14
  36.5 2.9 copy-start.42
  36.5 2.9 copy-start.43
  36.5 2.9 copy-start.44
  36.5 2.9 copy-start.45
  36.5 2.9 copy-start.46
  93.4 2.2 copy-start.2
  93.4 2.2 copy-start.47
  96.0 2.4 copy-start.4
  96.0 2.4 copy-start.7
  96.0 2.4 copy-start.48
  98.4 5.1 %copy-start.49 = (f32[1024,2048]{1,0:T(8,128)}, f32[1024,2048]{1,0:T(8,128)S(1)}, u32[]{:S(2)}) copy-start(f32[1024,2048]{1,0:T(8,128)S(1)} %fusion.117) | copy-start | bytes 25165828
  103.5 3.4 copy-start.3
  103.5 3.6 %copy-start.1 = (f32[14,134,512]{2,1,0:T(8,128)S(1)}, f32[14,134,512]{2,1,0:T(8,128)}, u32[]{:S(2)}) copy-start(f32[14,134,512]{2,1,0:T(8,128)} %maximum_convert_fusion) | copy-start | bytes 11526148
  130.1 23.3 %collective-permute-start.5 = (bf16[3,128,512]{2,1,0:T(8,128)(2,1)}, bf16[3,128,512]{2,1,0:T(8,128)(2,1)S(1)}, u32[]{:S(2)}, u32[]{:S(2)}) collective-permute-start(bf16[3,128,512]{2,1,0:T(8,128)(2,1)} %bitcast.55), channel_id=1, source_target_pairs={{4,0},{8,4},{12,8},{16,12},{20,16},{24,20},{28,24},{5,1},{9,5},{13... | collective-permute-start | bytes 1179656 | tf_op jit(solution)/shard_map/ppermute | solution.py:17
  131.4 22.2 %collective-permute-start.4 = (bf16[3,128,512]{2,1,0:T(8,128)(2,1)}, bf16[3,128,512]{2,1,0:T(8,128)(2,1)}, u32[]{:S(2)}, u32[]{:S(2)}) collective-permute-start(bf16[3,128,512]{2,1,0:T(8,128)(2,1)} %bitcast.53), channel_id=1, source_target_pairs={{0,4},{4,8},{8,12},{12,16},{16,20},{20,24},{24,28},{1,5},{5,9},{9,... | collective-permute-start | bytes 1179656 | tf_op jit(solution)/shard_map/ppermute | solution.py:14
  155.1 49.5 %collective-permute-start.7 = (bf16[14,3,512]{2,1,0:T(4,128)(2,1)}, bf16[14,3,512]{2,1,0:T(4,128)(2,1)}, u32[]{:S(2)}, u32[]{:S(2)}) collective-permute-start(bf16[14,3,512]{2,1,0:T(4,128)(2,1)} %get-tuple-element.64), channel_id=1, source_target_pairs={{1,0},{2,1},{3,2},{5,4},{6,5},{7,6},{9,8},{10,9},{11,10},{13,12},{... | collective-permute-start | bytes 129032 | tf_op jit(solution)/shard_map/ppermute | solution.py:17
  156.3 48.2 %collective-permute-start.6 = (bf16[14,3,512]{2,1,0:T(4,128)(2,1)}, bf16[14,3,512]{2,1,0:T(4,128)(2,1)}, u32[]{:S(2)}, u32[]{:S(2)}) collective-permute-start(bf16[14,3,512]{2,1,0:T(4,128)(2,1)} %get-tuple-element.63), channel_id=1, source_target_pairs={{0,1},{1,2},{2,3},{4,5},{5,6},{6,7},{8,9},{9,10},{10,11},{12,13},{... | collective-permute-start | bytes 129032 | tf_op jit(solution)/shard_map/ppermute | solution.py:14
  339.7 4.9 %copy-start.5 = (f32[2048,512]{1,0:T(8,128)S(1)}, f32[2048,512]{1,0:T(8,128)}, u32[]{:S(2)}) copy-start(f32[2048,512]{1,0:T(8,128)} %get-tuple-element.129) | copy-start | bytes 12582916
Sparse Core Ops, SparseCore 0:
  153.6 184.5 all-reduce.2
where the time goes:
time: 354 us; the launch traced here: 353 us
  other arithmetic  132 us (37%)
  waiting for transfers between devices  90.8 us (26%)
  blocking collectives  44.4 us (13%)
  local copies, waits for them, and re-layouts  24.7 us (7%)
  matrix products  23.8 us (7%)
  starting transfers between devices  22.8 us (6%)
  between operations  14.9 us (4%)
    psum x1, waiting for transfers between devices, on_device(): lax.psum((grad_up, grad_down, grad_dw, grad_gain), ('rows', 'cols'))  77.8 us
    reduce_sum x1, other arithmetic, pointwise(): mean = jnp.mean(conv, axis=-1, keepdims=True)  54 us
    convert_element_type x1, other arithmetic, on_device(): grad_input = total.astype(jnp.bfloat16)  52.3 us
    psum x1, blocking collectives, on_device(): lax.psum((grad_up, grad_down, grad_dw, grad_gain), ('rows', 'cols'))  44.4 us
    ppermute x4, starting transfers between devices, padded_2(): lax.ppermute(lax.slice_in_dim(block, block.shape[dim] - width, None, axis...  17.6 us
    reduce_sum x3, other arithmetic, on_device(): jnp.sum(padded[tap_i:tap_i + rows, tap_j:tap_j + cols] * grad_f, axis=(0,...  15.9 us
    ppermute x4, waiting for transfers between devices, padded_2(): lax.ppermute(lax.slice_in_dim(block, block.shape[dim] - width, None, axis...  13 us
    another operation x1, local copies, waits for them, and re-layouts, on_device(): grad_dw = jnp.stack(taps)  9.36 us
  transfers between devices with their start and end apart: 9, of which 3 were waited for; matrix products, arithmetic and copies ran while one was open for 22% of the time, Pallas kernels for 0%

commit v1 on v0

--- a/solution.py
+++ b/solution.py
@@ -100,8 +100,8 @@
                 * dw_weight[7 * tap_i + tap_j]
             )
     grad_input = total.astype(jnp.bfloat16)
-    grad_up, grad_down, grad_dw, grad_gain = lax.psum(
-        (grad_up, grad_down, grad_dw, grad_gain), ("rows", "cols")
+    grad_up, grad_down, grad_dw, grad_gain = jax.lax.psum(
+        jax.lax.psum((grad_up, grad_down, grad_dw, grad_gain), "cols"), "rows"
     )
     return (grad_input, grad_dw, grad_gain, grad_up, grad_down)
 

time: 354 us -> 595 us (1.68)
  waiting for transfers between devices: 90.8 us -> 360 us
  blocking collectives: 44.4 us -> 28.7 us
    psum x1 -> x2, waiting for transfers between devices: 77.8 us -> 323 us  [the longest x1 164 us: on_device(): jax.lax.psum(jax.lax.psum((grad_up, grad_down, grad_dw, grad_gain), 'cols...]
    ppermute x4, waiting for transfers between devices: 13 us -> 29 us  [padded_2(): lax.ppermute(lax.slice_in_dim(block, block.shape[dim] - width, None, axis...]
    psum x1 -> x2, blocking collectives: 44.4 us -> 28.7 us  [the longest x1 21.5 us: on_device(): jax.lax.psum(jax.lax.psum((grad_up, grad_down, grad_dw, grad_gain), 'cols...]
    ppermute x4, waiting for transfers between devices: 0.01 us -> 7.6 us  [padded_2(): lax.ppermute(lax.slice_in_dim(block, 0, width, axis=dim), axis, backward)]
  transfers between devices with their start and end apart: 9 -> 10, of which waited for: 3 -> 5; matrix products, arithmetic and copies ran while one was open for 22% -> 10% of each run, Pallas kernels for 0% -> 0%
where the time goes in v1:
time: 595 us; the launch traced here: 594 us
  waiting for transfers between devices  360 us (61%)
  other arithmetic  131 us (22%)
  blocking collectives  28.7 us (5%)
  matrix products  20.9 us (4%)
  starting transfers between devices  20.8 us (3%)
  local copies, waits for them, and re-layouts  18.9 us (3%)
  between operations  14.4 us (2%)
    psum x1, waiting for transfers between devices, on_device(): jax.lax.psum(jax.lax.psum((grad_up, grad_down, grad_dw, grad_gain), 'cols...  164 us
    psum x1, waiting for transfers between devices, on_device(): jax.lax.psum((grad_up, grad_down, grad_dw, grad_gain), 'cols')  159 us
    reduce_sum x1, other arithmetic, pointwise(): mean = jnp.mean(conv, axis=-1, keepdims=True)  55.9 us
    convert_element_type x1, other arithmetic, on_device(): grad_input = total.astype(jnp.bfloat16)  52.9 us
    ppermute x4, waiting for transfers between devices, padded_2(): lax.ppermute(lax.slice_in_dim(block, block.shape[dim] - width, None, axis...  29 us
    psum x1, blocking collectives, on_device(): jax.lax.psum(jax.lax.psum((grad_up, grad_down, grad_dw, grad_gain), 'cols...  21.5 us
    ppermute x4, starting transfers between devices, padded_2(): lax.ppermute(lax.slice_in_dim(block, block.shape[dim] - width, None, axis...  15.6 us
    reduce_sum x3, other arithmetic, on_device(): jnp.sum(padded[tap_i:tap_i + rows, tap_j:tap_j + cols] * grad_f, axis=(0,...  14.3 us
  transfers between devices with their start and end apart: 10, of which 5 were waited for; matrix products, arithmetic and copies ran while one was open for 10% of the time, Pallas kernels for 0%

profile of v1, /device:TPU:0, one launch (start us, length us, event | category | flops | bytes accessed | tf_op | source)
XLA Modules:
  0.0 594.0 jit_solution(7654602855492389848)
XLA Ops:
  7.2 0.0 copy-start
  7.2 0.0 copy-start.5
  7.2 0.0 all-reduce.7.cloned.1.call-start
  7.2 1.4 fusion.113
  8.6 4.9 collective-permute-start
  13.5 1.3 collective-permute-start.1
  14.8 1.1 fusion.114
  15.9 1.2 fusion.115
  17.1 13.2 %collective-permute-done = bf16[3,128,512]{2,1,0:T(8,128)(2,1)S(1)} collective-permute-done((bf16[3,128,512]{2,1,0:T(8,128)(2,1)S(1)}, bf16[3,128,512]{2,1,0:T(8,128)(2,1)S(1)}, u32[]{:S(2)}, u32[]{:S(2)}) %collective-permute-start) | collective-permute-done | bytes 393248 | tf_op jit(solution)/shard_map/ppermute | solution.py:14
  30.3 0.0 copy-done.5
  30.3 0.1 constant_dynamic-update-slice_fusion.1
  30.4 0.0 collective-permute-done.1
  30.6 1.3 collective-permute-start.3
  31.9 3.0 collective-permute-start.2
  34.9 1.0 fusion.116
  35.9 0.0 collective-permute-done.3
  35.9 0.0 collective-permute-done.2
  35.9 2.5 maximum_convert_fusion
  38.4 55.9 %fusion.110 = (f32[8,128]{1,0:T(8,128)S(1)}, f32[8,128,512]{2,1,0:T(8,128)}) fusion(f32[512]{0:T(512)S(1)} %bitcast.277, f32[14,134,512]{2,1,0:T(8,128)} %maximum_convert_fusion, f32[512]{0:T(512)S(1)} %bitcast.279, f32[512]{0:T(512)S(1)} %bitcast.185, f32[512]{0:T(512)S(1)} %bitcast.187, f32[512]{0:T(512)S(1)} %bitcast.189, f32[512]{0:T(512)S(1)} %bitcast.191, ...), kind=kLoop, calls=%fused_computation.231 | loop fusion | flops 51379200 | bytes 104962048 | tf_op jit(solution)/shard_map/reduce_sum | solution.py:34
  94.3 0.0 copy-start.3
  94.3 0.0 copy-start.7
  94.3 2.1 multiply_reduce_fusion.2
  96.5 0.0 copy-done.3
  96.5 0.0 copy-done.7
  96.5 0.3 multiply_convert_fusion.3
  96.9 0.0 copy-done
  96.9 0.0 copy-start.6
  96.9 0.0 copy-start.8
  96.9 2.3 fusion.117
  99.3 0.0 copy-start.9
  99.3 0.0 copy-done.6
  99.3 0.0 copy-done.8
  99.3 5.0 fusion.5
  104.4 0.0 copy-start.2
  104.4 2.9 multiply_reduce_fusion
  107.2 0.0 copy-done.2
  107.2 6.2 %fusion.56 = (f32[512]{0:T(512)S(1)}, f32[512]{0:T(512)S(1)}, f32[512]{0:T(512)S(1)}, f32[512]{0:T(512)S(1)}, f32[512]{0:T(512)S(1)}, /*index=5*/f32[512]{0:T(51...) fusion(f32[14,134,512]{2,1,0:T(8,128)S(1)} %copy-done.2, ...), kind=kLoop, calls=%fused_computation.108 | loop fusion | flops 23583744 | bytes 43046912 | tf_op jit(solution)/shard_map/reduce_sum | solution.py:90
  113.5 3.4 fusion.20
  116.9 4.7 fusion.38
  121.5 4.5 fusion.118
  126.0 6.2 %fusion.6 = f32[2048,512]{1,0:T(8,128)} fusion(bf16[1024,512]{1,0:T(8,128)(2,1)S(1)} %bitcast.180, f32[1024,2048]{1,0:T(8,128)} %copy-done.9), kind=kOutput, calls=%fused_computation.58 | convolution fusion | flops 2157969408 | bytes 13631488 | tf_op jit(solution)/shard_map/dot_general | solution.py:42
  132.2 4.4 stack.199
  136.6 0.0 all-reduce.7.cloned.1.call-update
  136.6 0.0 all-reduce.5.cloned.1.call-start
  136.7 159.3 %all-reduce.7.cloned.1.call-done = (f32[49,512]{1,0:T(8,128)}, f32[512,2048]{1,0:T(8,128)}, f32[2048,512]{1,0:T(8,128)}) async-done(((f32[49,512]{1,0:T(8,128)}, f32[512,2048]{1,0:T(8,128)}, f32[2048,512]{1,0:T(8,128)}), (f32[49,512]{1,0:T(8,128)}, f32[512,2048]{1,0:T(8,128)}, f32[2048,512]{1,0:T(8,128)})) %all-reduce.7.cloned.1.call-update) | async-done | bytes 8488976 | tf_op jit(solution)/shard_map/psum | solution.py:104
  295.9 0.0 all-reduce.5.cloned.1.call-update
  296.0 0.1 fusion.112
  296.0 1.3 collective-permute-start.5
  297.3 4.6 collective-permute-start.4
  301.9 7.6 %collective-permute-done.5 = bf16[3,128,512]{2,1,0:T(8,128)(2,1)S(1)} collective-permute-done((bf16[3,128,512]{2,1,0:T(8,128)(2,1)S(1)}, bf16[3,128,512]{2,1,0:T(8,128)(2,1)S(1)}, u32[]{:S(2)}, u32[]{:S(2)}) %collective-permute-start.5) | collective-permute-done | bytes 393248 | tf_op jit(solution)/shard_map/ppermute | solution.py:17
  309.5 15.8 %collective-permute-done.4 = bf16[3,128,512]{2,1,0:T(8,128)(2,1)S(1)} collective-permute-done((bf16[3,128,512]{2,1,0:T(8,128)(2,1)S(1)}, bf16[3,128,512]{2,1,0:T(8,128)(2,1)S(1)}, u32[]{:S(2)}, u32[]{:S(2)}) %collective-permute-start.4) | collective-permute-done | bytes 393248 | tf_op jit(solution)/shard_map/ppermute | solution.py:14
  325.3 1.3 collective-permute-start.7
  326.6 3.0 collective-permute-start.6
  329.7 7.1 %psum.58 = f32[512]{0:T(512)S(1)} all-reduce(f32[512]{0:T(512)S(1)} %get-tuple-element.54), channel_id=1, replica_groups=mesh['rows'=8,'cols'=4] {'cols'}, use_global_device_ids=true, to_apply=%region_56.0 | all-reduce | flops 512 | bytes 4096 | tf_op jit(solution)/shard_map/psum | solution.py:104
  336.8 21.5 %psum.59 = f32[512]{0:T(512)} all-reduce(f32[512]{0:T(512)S(1)} %psum.58), channel_id=1, replica_groups=mesh['rows'=8,'cols'=4] {'rows'}, use_global_device_ids=true, to_apply=%region_57.0 | all-reduce | flops 512 | bytes 4096 | tf_op jit(solution)/shard_map/psum | solution.py:103
  358.3 0.0 collective-permute-done.7
  358.3 0.0 collective-permute-done.6
  358.3 2.5 maximum_convert_fusion.1
  360.9 52.9 %fusion.58 = bf16[8,128,512]{2,1,0:T(8,128)(2,1)} fusion(f32[14,134,512]{2,1,0:T(8,128)} %maximum_convert_fusion.1, bf16[8,128,512]{2,1,0:T(8,128)(2,1)S(1)} %copy-done.6, f32[512]{0:T(512)S(1)} %bitcast.278, f32[512]{0:T(512)S(1)} %bitcast.280, f32[512]{0:T(512)S(1)} %bitcast.186, f32[512]{0:T(512)S(1)} %bitcast.188, f32[512]{0:T(512)S(1)} %bitcast.190, ...), kind=kLoop, calls=%fused_computation.111 | loop fusion | flops 52428800 | bytes 104957952 | tf_op jit(solution)/shard_map/convert_element_type | solution.py:102
  413.7 163.9 %all-reduce.5.cloned.1.call-done = (f32[49,512]{1,0:T(8,128)}, f32[512,2048]{1,0:T(8,128)}, f32[2048,512]{1,0:T(8,128)}) async-done(((f32[49,512]{1,0:T(8,128)}, f32[512,2048]{1,0:T(8,128)}, f32[2048,512]{1,0:T(8,128)}), (f32[49,512]{1,0:T(8,128)}, f32[512,2048]{1,0:T(8,128)}, f32[2048,512]{1,0:T(8,128)})) %all-reduce.5.cloned.1.call-update) | async-done | bytes 8488976 | tf_op jit(solution)/shard_map/psum | solution.py:103
  577.7 1.6 copy.19
  579.2 4.8 copy.20
  584.1 2.1 copy.21
  586.2 1.0 copy-done.1
  (11 shorter events, 0.2 us)
Async XLA Ops:
  7.2 89.7 %copy-start = (bf16[512,2048]{1,0:T(8,128)(2,1)S(1)}, bf16[512,2048]{1,0:T(8,128)(2,1)}, u32[]{:S(2)}) copy-start(bf16[512,2048]{1,0:T(8,128)(2,1)} %param.9) | copy-start | bytes 6291460
  7.2 23.1 %copy-start.5 = (bf16[8,128,512]{2,1,0:T(8,128)(2,1)S(1)}, bf16[8,128,512]{2,1,0:T(8,128)(2,1)}, u32[]{:S(2)}) copy-start(bf16[8,128,512]{2,1,0:T(8,128)(2,1)} %param.6) | copy-start | bytes 3145732
  7.2 288.8 %all-reduce.7.cloned.1.call-start = ((), (), s32[]{:S(2)}) async-start(), calls=%async_computation.1 | async-start | bytes 17006592 | tf_op jit(solution)/shard_map/psum | solution.py:104
  8.6 21.7 %collective-permute-start = (bf16[3,128,512]{2,1,0:T(8,128)(2,1)S(1)}, bf16[3,128,512]{2,1,0:T(8,128)(2,1)S(1)}, u32[]{:S(2)}, u32[]{:S(2)}) collective-permute-start(bf16[3,128,512]{2,1,0:T(8,128)(2,1)S(1)} %get-tuple-element.73), channel_id=1, source_target_pairs={{0,4},{4,8},{8,12},{12,16},{16,20},{20,24},{24,28},{1,5},{5,9},{9,... | collective-permute-start | bytes 1179656 | tf_op jit(solution)/shard_map/ppermute | solution.py:14
  13.5 16.9 %collective-permute-start.1 = (bf16[3,128,512]{2,1,0:T(8,128)(2,1)S(1)}, bf16[3,128,512]{2,1,0:T(8,128)(2,1)S(1)}, u32[]{:S(2)}, u32[]{:S(2)}) collective-permute-start(bf16[3,128,512]{2,1,0:T(8,128)(2,1)S(1)} %get-tuple-element.72), channel_id=1, source_target_pairs={{4,0},{8,4},{12,8},{16,12},{20,16},{24,20},{28,24},{5,1},{9,5},{13... | collective-permute-start | bytes 1179656 | tf_op jit(solution)/shard_map/ppermute | solution.py:17
  30.6 5.3 collective-permute-start.3
  31.9 4.0 collective-permute-start.2
  94.3 2.2 copy-start.3
  94.3 2.2 copy-start.7
  96.9 2.4 copy-start.6
  96.9 2.4 copy-start.8
  99.3 5.1 copy-start.9
  104.4 2.9 copy-start.2
  136.6 441.0 %all-reduce.5.cloned.1.call-start = ((), (), s32[]{:S(2)}) async-start(), calls=%async_computation | async-start | bytes 17006592 | tf_op jit(solution)/shard_map/psum | solution.py:103
  296.0 13.5 %collective-permute-start.5 = (bf16[3,128,512]{2,1,0:T(8,128)(2,1)S(1)}, bf16[3,128,512]{2,1,0:T(8,128)(2,1)S(1)}, u32[]{:S(2)}, u32[]{:S(2)}) collective-permute-start(bf16[3,128,512]{2,1,0:T(8,128)(2,1)S(1)} %bitcast.182), channel_id=1, source_target_pairs={{4,0},{8,4},{12,8},{16,12},{20,16},{24,20},{28,24},{5,1},{9,5},{13... | collective-permute-start | bytes 1179656 | tf_op jit(solution)/shard_map/ppermute | solution.py:17
  297.3 28.0 %collective-permute-start.4 = (bf16[3,128,512]{2,1,0:T(8,128)(2,1)S(1)}, bf16[3,128,512]{2,1,0:T(8,128)(2,1)S(1)}, u32[]{:S(2)}, u32[]{:S(2)}) collective-permute-start(bf16[3,128,512]{2,1,0:T(8,128)(2,1)S(1)} %bitcast.181), channel_id=1, source_target_pairs={{0,4},{4,8},{8,12},{12,16},{16,20},{20,24},{24,28},{1,5},{5,9},{9,... | collective-permute-start | bytes 1179656 | tf_op jit(solution)/shard_map/ppermute | solution.py:14
  325.3 33.0 %collective-permute-start.7 = (bf16[14,3,512]{2,1,0:T(4,128)(2,1)S(1)}, bf16[14,3,512]{2,1,0:T(4,128)(2,1)S(1)}, u32[]{:S(2)}, u32[]{:S(2)}) collective-permute-start(bf16[14,3,512]{2,1,0:T(4,128)(2,1)S(1)} %get-tuple-element.67), channel_id=1, source_target_pairs={{1,0},{2,1},{3,2},{5,4},{6,5},{7,6},{9,8},{10,9},{11,10},{13,12},{... | collective-permute-start | bytes 129032 | tf_op jit(solution)/shard_map/ppermute | solution.py:17
  326.6 31.7 %collective-permute-start.6 = (bf16[14,3,512]{2,1,0:T(4,128)(2,1)S(1)}, bf16[14,3,512]{2,1,0:T(4,128)(2,1)S(1)}, u32[]{:S(2)}, u32[]{:S(2)}) collective-permute-start(bf16[14,3,512]{2,1,0:T(4,128)(2,1)S(1)} %get-tuple-element.66), channel_id=1, source_target_pairs={{0,1},{1,2},{2,3},{4,5},{5,6},{6,7},{8,9},{9,10},{10,11},{12,13},{... | collective-permute-start | bytes 129032 | tf_op jit(solution)/shard_map/ppermute | solution.py:14
  579.2 4.9 copy-start.4
  584.1 3.1 copy-start.1
Sparse Core Ops, SparseCore 0:
  136.8 159.1 all-reduce.6
  300.5 277.1 all-reduce.4
